TPU v7x, 32 devices: a whole 2x2x4 slice. The times are simulated.
32 devices in a mesh: row: 4 (over y, core), col: 8 (over z, x).
Axes of the slice: x: 2, y: 2, z: 4, core: 2. Of those that a mesh axis runs over, the one named last changes fastest.
Arguments:
- tokens: bfloat16 [40, 8192], P('col', 'row'), may hold values from -6 to 6
- grad_out: bfloat16 [40, 8192], P('col', 'row'), may hold values from -6 to 6
- gate_weight: bfloat16 [8192, 28672], P('row', 'col'), may hold values from -0.0625 to 0.0625
- up_weight: bfloat16 [8192, 28672], P('row', 'col'), may hold values from -0.0625 to 0.0625
- down_weight: bfloat16 [28672, 8192], P('col', 'row'), may hold values from -0.03125 to 0.03125
Outputs:
- grad_tokens: bfloat16 [40, 8192], P('col', 'row')
- grad_gate_weight: bfloat16 [8192, 28672], P('row', 'col')
- grad_up_weight: bfloat16 [8192, 28672], P('row', 'col')
- grad_down_weight: bfloat16 [28672, 8192], P('col', 'row')
All inputs are finite; a program needn't handle non-finite values.
Results may differ from a plain program's by a relative error of at most 0.0049.
Values may be sent and summed in bfloat16 or wider, within the bound.
A program may use at most 192 MiB of HBM per device.

v0:
```python
import functools

import jax
import jax.numpy as jnp
from jax import lax
from jax.experimental import pallas as pl
from jax.experimental.pallas import tpu as pltpu
from jax.sharding import PartitionSpec as P

F32 = jnp.float32
BF16 = jnp.bfloat16
LAST = (((1,), (1,)), ((), ()))
MESH = pl.DeviceIdType.MESH


def hidden_grads(gate_sum, up_sum, back_sum):
    sigmoid_gate = 1.0 / (1.0 + jnp.exp(-gate_sum))
    activated = gate_sum * sigmoid_gate
    hidden = (activated * up_sum).astype(BF16)
    grad_up = (back_sum * activated).astype(BF16)
    slope = sigmoid_gate * (1.0 + gate_sum * (1.0 - sigmoid_gate))
    grad_gate = (back_sum * up_sum * slope).astype(BF16)
    return (hidden, grad_gate, grad_up)


def exchange_kernel(
    rows, cols, tok_in, grad_in, gate_hbm, up_hbm, down_hbm,
    tok_out, grad_out, acts_out, dtok_out,
    gate_buf, up_buf, down_buf, tok_slots, grad_slots, stage, tok_all, grad_all,
    part_send, part_recv, acts, acc, dtok_send, dtok_recv,
    load_sem, own_sem, tok_ssem, tok_rsem, part_ssem, part_rsem,
    acts_ssem, acts_rsem, fwd_ssem, fwd_rsem, dtok_ssem, dtok_rsem, out_sem,
):
    row, col = lax.axis_index("row"), lax.axis_index("col")
    chips = rows // 2
    chip, core = row // 2, row % 2
    width = gate_buf.shape[2]
    few = tok_in.shape[0]

    def peer(dy, dc):
        return ((chip + dy) % chips) * 2 + (core + dc) % 2

    offsets = [(dy, dc) for dy in range(1, chips) for dc in (0, 1)] + [(0, 1), (0, 0)]

    loads = []
    for o, (dy, dc) in enumerate(offsets):
        at = pl.multiple_of(peer(dy, dc) * width, 128)
        trio = (
            pltpu.make_async_copy(gate_hbm.at[:, pl.ds(at, width)], gate_buf.at[o], load_sem.at[0, o]),
            pltpu.make_async_copy(up_hbm.at[:, pl.ds(at, width)], up_buf.at[o], load_sem.at[1, o]),
            pltpu.make_async_copy(down_hbm.at[pl.ds(at, width), :], down_buf.at[o], load_sem.at[2, o]),
        )
        loads.append(trio)
    for load in loads[0]:
        load.start()

    barrier = pltpu.get_barrier_semaphore()
    for dy, dc in offsets[:-1]:
        pl.semaphore_signal(barrier, inc=1, device_id=(peer(dy, dc), col), device_id_type=MESH)
    for s in range(1, cols):
        pl.semaphore_signal(barrier, inc=1, device_id=(row, (col + s) % cols), device_id_type=MESH)
    own_tok = pltpu.make_async_copy(tok_in, tok_slots.at[col], own_sem.at[0])
    own_grad = pltpu.make_async_copy(grad_in, grad_slots.at[col], own_sem.at[1])
    own_tok.start()
    own_grad.start()
    pl.semaphore_wait(barrier, rows - 1 + cols - 1)

    def gather(s, slot):
        to = (row, (col + s) % cols)
        return [
            pltpu.make_async_remote_copy(
                src_ref=src, dst_ref=dst.at[slot], send_sem=tok_ssem.at[a, s], recv_sem=tok_rsem.at[a, s],
                device_id=to, device_id_type=MESH,
            )
            for a, (src, dst) in enumerate(((tok_in, tok_slots), (grad_in, grad_slots)))
        ]

    for s in range(1, cols):
        for copy in gather(s, col):
            copy.start()
    for trio in loads[1:]:
        for load in trio:
            load.start()
    own_tok.wait()
    own_grad.wait()
    for s in range(1, cols):
        for copy in gather(s, (col + cols - s) % cols):
            copy.wait_recv()
    for slots, whole in ((tok_slots, tok_all), (grad_slots, grad_all)):
        for k in range(cols):
            stage[k * few : (k + 1) * few, :] = slots[k].astype(F32)
        whole[...] = stage[...].astype(BF16)
    outs = [
        pltpu.make_async_copy(tok_all, tok_out, out_sem.at[0]),
        pltpu.make_async_copy(grad_all, grad_out, out_sem.at[1]),
    ]
    for copy in outs:
        copy.start()

    def partial(o):
        for load in loads[o]:
            load.wait()
        gate_part = jnp.dot(tok_all[...], gate_buf[o], preferred_element_type=F32)
        up_part = jnp.dot(tok_all[...], up_buf[o], preferred_element_type=F32)
        back_part = lax.dot_general(down_buf[o], grad_all[...], LAST, preferred_element_type=F32).T
        return gate_part, up_part, back_part

    sends = []
    for o, (dy, dc) in enumerate(offsets[:-1]):
        for i, part in enumerate(partial(o)):
            part_send[o, i] = part.astype(BF16)
        copy = pltpu.make_async_remote_copy(
            src_ref=part_send.at[o], dst_ref=part_recv.at[o],
            send_sem=part_ssem.at[o], recv_sem=part_rsem.at[o],
            device_id=(peer(dy, dc), col), device_id_type=MESH,
        )
        copy.start()
        sends.append(copy)
    last = rows - 1
    sums = list(partial(last))
    for o in range(rows - 1):
        sends[o].wait_recv()
        sums = [total + part_recv[o, i].astype(F32) for i, total in enumerate(sums)]
    for i, value in enumerate(hidden_grads(*sums)):
        acts[row, i] = value

    def share(sems, n, q, to):
        return pltpu.make_async_remote_copy(
            src_ref=acts.at[q], dst_ref=acts.at[q], send_sem=sems[0].at[n], recv_sem=sems[1].at[n],
            device_id=(to, col), device_id_type=MESH,
        )

    direct, forward = (acts_ssem, acts_rsem), (fwd_ssem, fwd_rsem)
    other = peer(0, 1)
    for dy in range(1, chips):
        share(direct, dy, row, peer(dy, 0)).start()
    share(forward, 0, row, other).start()

    block = acc.shape[0] // 4

    def add_block(o, q, first):
        @pl.loop(0, 4)
        def _(t):
            at = pl.ds(pl.multiple_of(t * block, block), block)
            value = lax.dot_general(gate_buf[o, at, :], acts[q, 1], LAST, preferred_element_type=F32)
            value += lax.dot_general(up_buf[o, at, :], acts[q, 2], LAST, preferred_element_type=F32)
            acc[at, :] = value if first else acc[at, :] + value

    add_block(last, row, True)
    share(forward, 0, other, other).wait_recv()
    add_block(last - 1, other, False)
    for dy in range(1, chips):
        q = peer(chips - dy, 0)
        share(direct, dy, q, peer(dy, 0)).wait_recv()
        share(forward, dy, q, other).start()
        add_block(2 * (chips - dy - 1), q, False)
    for dy in range(1, chips):
        q = peer(chips - dy, 1)
        share(forward, dy, q, other).wait_recv()
        add_block(2 * (chips - dy - 1) + 1, q, False)

    total = acc[...].T
    stage[...] = total
    for k in range(cols):
        dtok_send[k] = stage[k * few : (k + 1) * few, :].astype(BF16)

    def scatter(s):
        to = (col + s) % cols
        return pltpu.make_async_remote_copy(
            src_ref=dtok_send.at[to], dst_ref=dtok_recv.at[s], send_sem=dtok_ssem.at[s],
            recv_sem=dtok_rsem.at[s], device_id=(row, to), device_id_type=MESH,
        )

    for s in range(1, cols):
        scatter(s).start()
    outs.append(pltpu.make_async_copy(acts, acts_out, out_sem.at[2]))
    outs[-1].start()
    result = dtok_send[col].astype(F32)
    for s in range(1, cols):
        scatter(s).wait_recv()
        result += dtok_recv[s].astype(F32)
    dtok_out[...] = result.astype(BF16)

    for copy in outs:
        copy.wait()
    for s in range(1, cols):
        for copy in gather(s, col):
            copy.wait_send()
        scatter(s).wait_send()
    for copy in sends:
        copy.wait_send()
    share(forward, 0, row, other).wait_send()
    for dy in range(1, chips):
        share(direct, dy, row, peer(dy, 0)).wait_send()
        share(forward, dy, peer(chips - dy, 0), other).wait_send()


def exchange(rows, cols, tokens, grad_out, gate_weight, up_weight, down_weight):
    few, depth = tokens.shape
    hidden = gate_weight.shape[1]
    width = hidden // rows
    many = few * cols
    dma = pltpu.SemaphoreType.DMA
    any_spec = pl.BlockSpec(memory_space=pl.ANY)
    vmem_spec = pl.BlockSpec(memory_space=pltpu.VMEM)
    shape = jax.ShapeDtypeStruct
    return pl.pallas_call(
        functools.partial(exchange_kernel, rows, cols),
        out_shape=(
            shape((many, depth), BF16),
            shape((many, depth), BF16),
            shape((rows, 3, many, width), BF16),
            shape((few, depth), BF16),
        ),
        in_specs=[vmem_spec, vmem_spec, any_spec, any_spec, any_spec],
        out_specs=(any_spec, any_spec, any_spec, vmem_spec),
        scratch_shapes=[
            pltpu.VMEM((rows, depth, width), BF16),
            pltpu.VMEM((rows, depth, width), BF16),
            pltpu.VMEM((rows, width, depth), BF16),
            pltpu.VMEM((cols, few, depth), BF16),
            pltpu.VMEM((cols, few, depth), BF16),
            pltpu.VMEM((many, depth), F32),
            pltpu.VMEM((many, depth), BF16),
            pltpu.VMEM((many, depth), BF16),
            pltpu.VMEM((rows - 1, 3, many, width), BF16),
            pltpu.VMEM((rows - 1, 3, many, width), BF16),
            pltpu.VMEM((rows, 3, many, width), BF16),
            pltpu.VMEM((depth, many), F32),
            pltpu.VMEM((cols, few, depth), BF16),
            pltpu.VMEM((cols, few, depth), BF16),
            dma((3, rows)),
            dma((2,)),
            dma((2, cols)),
            dma((2, cols)),
            dma((rows,)),
            dma((rows,)),
            dma((rows,)),
            dma((rows,)),
            dma((rows,)),
            dma((rows,)),
            dma((cols,)),
            dma((cols,)),
            dma((3,)),
        ],
        compiler_params=pltpu.CompilerParams(
            collective_id=0, has_side_effects=True, vmem_limit_bytes=62 * 1024 * 1024
        ),
        name="exchange",
    )(tokens, grad_out, gate_weight, up_weight, down_weight)


def outer_kernel(tok, grad, acts, gate_out, up_out, down_out, hidden_t):
    rows, _, _, width = acts.shape

    @pl.when(pl.program_id(0) == 0)
    def _():
        for q in range(rows):
            hidden_t[q * width : (q + 1) * width, :] = acts[q, 0].astype(F32).T.astype(BF16)

    tok_t = tok[...].astype(F32).T.astype(BF16)
    for out, i in ((gate_out, 1), (up_out, 2)):
        @pl.loop(0, rows)
        def _(q):
            at = pl.ds(pl.multiple_of(q * width, 128), width)
            out[:, at] = jnp.dot(tok_t, acts[q, i], preferred_element_type=F32).astype(BF16)

    @pl.loop(0, 2 * rows)
    def _(t):
        at = pl.ds(pl.multiple_of(t * (width // 2), 64), width // 2)
        down_out[at, :] = jnp.dot(hidden_t[at, :], grad[...], preferred_element_type=F32).astype(BF16)


def outer(tok, grad, acts):
    many, depth = tok.shape
    rows, _, _, width = acts.shape
    hidden = rows * width
    steps = 8
    while depth % (steps * 128):
        steps //= 2
    part = depth // steps
    shape = jax.ShapeDtypeStruct
    return pl.pallas_call(
        outer_kernel,
        grid=(steps,),
        out_shape=(
            shape((depth, hidden), BF16),
            shape((depth, hidden), BF16),
            shape((hidden, depth), BF16),
        ),
        in_specs=[
            pl.BlockSpec((many, part), lambda i: (0, i)),
            pl.BlockSpec((many, part), lambda i: (0, i)),
            pl.BlockSpec((rows, 3, many, width), lambda i: (0, 0, 0, 0)),
        ],
        out_specs=(
            pl.BlockSpec((part, hidden), lambda i: (i, 0)),
            pl.BlockSpec((part, hidden), lambda i: (i, 0)),
            pl.BlockSpec((hidden, part), lambda i: (0, i)),
        ),
        scratch_shapes=[pltpu.VMEM((hidden, many), BF16)],
        compiler_params=pltpu.CompilerParams(
            dimension_semantics=("arbitrary",), vmem_limit_bytes=40 * 1024 * 1024
        ),
        name="outer",
    )(tok, grad, acts)


def shards(rows, cols, tokens, grad_out, gate_weight, up_weight, down_weight):
    tok, grad, acts, grad_tokens = exchange(
        rows, cols, tokens, grad_out, gate_weight, up_weight, down_weight
    )
    return (grad_tokens, *outer(tok, grad, acts))


def plain_shards(tokens, grad_out, gate_weight, up_weight, down_weight):
    tok_full, grad_full = (
        lax.all_gather(tokens, "col", axis=0, tiled=True),
        lax.all_gather(grad_out, "col", axis=0, tiled=True),
    )
    hidden_width = gate_weight.shape[1]
    gate_part = jnp.dot(tok_full, gate_weight, preferred_element_type=F32)
    up_part = jnp.dot(tok_full, up_weight, preferred_element_type=F32)
    back_part = jnp.einsum("td,fd->tf", grad_full, down_weight, preferred_element_type=F32)
    sums = lax.psum(jnp.concatenate([gate_part, up_part, back_part], axis=1), "row")
    hidden, grad_gate, grad_up = hidden_grads(*jnp.split(sums, 3, axis=1))
    grad_down_weight = jnp.einsum("tf,td->fd", hidden, grad_full, preferred_element_type=F32).astype(BF16)
    grad_gate_weight = jnp.einsum("td,tf->df", tok_full, grad_gate, preferred_element_type=F32).astype(BF16)
    grad_up_weight = jnp.einsum("td,tf->df", tok_full, grad_up, preferred_element_type=F32).astype(BF16)
    total = jnp.einsum("tf,df->td", grad_gate, gate_weight, preferred_element_type=F32)
    total += jnp.einsum("tf,df->td", grad_up, up_weight, preferred_element_type=F32)
    grad_tokens = lax.psum_scatter(total, "col", scatter_dimension=0, tiled=True).astype(BF16)
    return (grad_tokens, grad_gate_weight, grad_up_weight, grad_down_weight)


def choose(rows, cols, *operands):
    depth, hidden = operands[2].shape
    if hidden % (rows * 128) or depth % 128 or rows % 2:
        return plain_shards(*operands)
    return shards(rows, cols, *operands)


def solution(mesh):
    placed = (P("col", "row"), P("col", "row"), P("row", "col"), P("row", "col"), P("col", "row"))
    return jax.shard_map(
        functools.partial(choose, mesh.shape["row"], mesh.shape["col"]),
        mesh=mesh,
        in_specs=placed,
        out_specs=(P("col", "row"), P("row", "col"), P("row", "col"), P("col", "row")),
        check_vma=False,
    )
```

profile of v0, /device:TPU:0, one launch (start us, length us, event | category | flops | bytes accessed | tf_op | source)
XLA Modules:
  0.0 87.9 jit_solution(17353706237036347008)
XLA Ops:
  0.6 50.7 %exchange.1 = (bf16[40,2048]{1,0:T(8,128)(2,1)}, bf16[40,2048]{1,0:T(8,128)(2,1)}, bf16[4,3,40,896]{3,2,1,0:T(8,128)(2,1)}, bf16[5,2048]{1,0:T(8,128)(2,1)}) custom-call(bf16[5,2048]{1,0:T(8,128)(2,1)} %tok_in.1, bf16[5,2048]{1,0:T(8,128)(2,1)} %grad_in.1, bf16[2048,3584]{1,0:T(8,128)(2,1)} %gate_hbm.1, bf16[2048,3584]{1,0:T(8,128)(2,1)} %up_hbm.1, ...), custom_call_target="tpu_custom_call" | custom-call | tf_op jit(solution)/shard_map/exchange/pallas_call | solution.py:207
  51.3 0.0 copy-start
  51.3 1.1 %copy-done = bf16[4,3,40,896]{3,2,1,0:T(8,128)(2,1)S(1)} copy-done((bf16[4,3,40,896]{3,2,1,0:T(8,128)(2,1)S(1)}, bf16[4,3,40,896]{3,2,1,0:T(8,128)(2,1)}, u32[]{:S(2)}) %copy-start) | copy-done | bytes 860184
  52.5 0.0 copy-start.1
  52.5 0.9 %copy-done.1 = bf16[40,2048]{1,0:T(8,128)(2,1)S(1)} copy-done((bf16[40,2048]{1,0:T(8,128)(2,1)S(1)}, bf16[40,2048]{1,0:T(8,128)(2,1)}, u32[]{:S(2)}) %copy-start.1) | copy-done | bytes 163864
  53.4 0.0 copy-start.2
  53.4 0.9 %copy-done.2 = bf16[40,2048]{1,0:T(8,128)(2,1)S(1)} copy-done((bf16[40,2048]{1,0:T(8,128)(2,1)S(1)}, bf16[40,2048]{1,0:T(8,128)(2,1)}, u32[]{:S(2)}) %copy-start.2) | copy-done | bytes 163864
  54.3 32.2 %outer.1 = (bf16[2048,3584]{1,0:T(8,128)(2,1)}, bf16[2048,3584]{1,0:T(8,128)(2,1)}, bf16[3584,2048]{1,0:T(8,128)(2,1)}) custom-call(bf16[40,2048]{1,0:T(8,128)(2,1)S(1)} %copy-done.1, bf16[40,2048]{1,0:T(8,128)(2,1)S(1)} %copy-done.2, bf16[4,3,40,896]{3,2,1,0:T(8,128)(2,1)S(1)} %copy-done), custom_call_target="tpu_custom_call" | custom-call | tf_op jit(solution)/shard_map/outer/pallas_call | solution.py:283
  86.5 1.4 %copy.10 = bf16[5,2048]{1,0:T(8,128)(2,1)} copy(bf16[5,2048]{1,0:T(8,128)(2,1)} %get-tuple-element.22) | data formatting | bytes 40960
Async XLA Ops:
  51.3 1.2 %copy-start = (bf16[4,3,40,896]{3,2,1,0:T(8,128)(2,1)S(1)}, bf16[4,3,40,896]{3,2,1,0:T(8,128)(2,1)}, u32[]{:S(2)}) copy-start(bf16[4,3,40,896]{3,2,1,0:T(8,128)(2,1)} %get-tuple-element.14.acts) | copy-start | bytes 2580484
  52.5 0.9 %copy-start.1 = (bf16[40,2048]{1,0:T(8,128)(2,1)S(1)}, bf16[40,2048]{1,0:T(8,128)(2,1)}, u32[]{:S(2)}) copy-start(bf16[40,2048]{1,0:T(8,128)(2,1)} %get-tuple-element.12.tok) | copy-start | bytes 491524
  53.4 0.9 %copy-start.2 = (bf16[40,2048]{1,0:T(8,128)(2,1)S(1)}, bf16[40,2048]{1,0:T(8,128)(2,1)}, u32[]{:S(2)}) copy-start(bf16[40,2048]{1,0:T(8,128)(2,1)} %get-tuple-element.13.grad) | copy-start | bytes 491524
where the time goes:
time: 88.2 us; the launch traced here: 87.9 us
  Pallas kernels  82.9 us (94%)
  local copies, waits for them, and re-layouts  4.36 us (5%)
    pallas_call x1, Pallas kernels, exchange(): pl.pallas_call(functools.partial(exchange_kernel, rows, cols), out_shape=...  50.7 us
    pallas_call x1, Pallas kernels, outer(): pl.pallas_call(outer_kernel, grid=(steps,), out_shape=(shape((depth, hidd...  32.2 us
    unnamed x7, local copies, waits for them, and re-layouts  4.36 us

commit v1 on v0

v1 whole, which is shorter than its diff:
```python
import functools

import jax
import jax.numpy as jnp
from jax import lax
from jax.experimental import pallas as pl
from jax.experimental.pallas import tpu as pltpu
from jax.sharding import PartitionSpec as P

F32 = jnp.float32
BF16 = jnp.bfloat16
LAST = (((1,), (1,)), ((), ()))
MESH = pl.DeviceIdType.MESH
HALF = 256
LANES = 128
LEAD = 2
DELAY = 3
PIECES = 2
TAIL = 2


def hidden_grads(gate_sum, up_sum, back_sum):
    sigmoid_gate = 1.0 / (1.0 + jnp.exp(-gate_sum))
    activated = gate_sum * sigmoid_gate
    hidden = (activated * up_sum).astype(BF16)
    grad_up = (back_sum * activated).astype(BF16)
    slope = sigmoid_gate * (1.0 + gate_sum * (1.0 - sigmoid_gate))
    grad_gate = (back_sum * up_sum * slope).astype(BF16)
    return (hidden, grad_gate, grad_up)


def exchange_kernel(
    rows, cols, tok_in, grad_in, gate_hbm, up_hbm, down_hbm,
    tok_out, grad_out, acts_out, dtok_out,
    gate_buf, up_buf, down_buf, tok_all, grad_all, packed, slots, loose, stage, parts, pair_recv,
    chip_send, chip_recv, acts, acc, dtok_send, dtok_recv,
    load_sem, line_ssem, line_rsem, fwd_ssem, fwd_rsem, pair_ssem, pair_rsem,
    chip_ssem, chip_rsem, acts_ssem, acts_rsem, dtok_ssem, dtok_rsem, out_sem, acts_sem,
):
    row, col = lax.axis_index("row"), lax.axis_index("col")
    chips, lines = rows // 2, cols // 2
    chip, core = row // 2, row % 2
    line, side = col // 2, col % 2
    few, depth = tok_in.shape
    half = acts.shape[-1]
    span = 2 * half
    chunks = acts.shape[0]
    strips = depth // LANES
    partner = chip * 2 + (1 - core)

    def remote(src, dst, ssem, rsem, to):
        return pltpu.make_async_remote_copy(
            src_ref=src, dst_ref=dst, send_sem=ssem, recv_sem=rsem, device_id=to, device_id_type=MESH
        )

    def load(i, k):
        at = pl.ds(k * span, span)
        if i == 2:
            return pltpu.make_async_copy(down_hbm.at[at, :], down_buf.at[at, :], load_sem.at[i, k])
        src, dst = ((gate_hbm, gate_buf), (up_hbm, up_buf))[i]
        return pltpu.make_async_copy(src.at[:, at], dst.at[:, at], load_sem.at[i, k])

    order = []
    for s in range(chunks + LEAD):
        if s < chunks:
            order += [(0, s), (1, s)]
        if s >= LEAD:
            order.append((2, s - LEAD))
    early = 2 * LEAD
    for i, k in order[:early]:
        load(i, k).start()

    barrier = pltpu.get_barrier_semaphore()
    for to in [partner] + [((chip + dy) % chips) * 2 + core for dy in range(1, chips)]:
        pl.semaphore_signal(barrier, inc=1, device_id=(to, col), device_id_type=MESH)
    for s in range(1, cols):
        pl.semaphore_signal(barrier, inc=1, device_id=(row, (col + s) % cols), device_id_type=MESH)
    for a, whole in enumerate((tok_in, grad_in)):
        for j in range(strips):
            loose[a, j * few : (j + 1) * few, :] = whole[:, j * LANES : (j + 1) * LANES].astype(F32)
        mine = loose[a].astype(BF16)
        packed[a] = mine
        slots[a, col] = mine
    pl.semaphore_wait(barrier, chips + cols - 1)

    def along(a, s):
        to = ((line + s) % lines) * 2 + side
        return remote(packed.at[a], slots.at[a, col], line_ssem.at[a, s], line_rsem.at[a, s], (row, to))

    def across(a, s):
        q = ((line + lines - s) % lines) * 2 + side
        src = packed.at[a] if s == 0 else slots.at[a, q]
        return remote(src, slots.at[a, q], fwd_ssem.at[a, s], fwd_rsem.at[a, s], (row, line * 2 + 1 - side))

    for a in range(2):
        for s in range(1, lines):
            along(a, s).start()
        across(a, 0).start()
    for i, k in order[early:]:
        load(i, k).start()
    for a in range(2):
        for s in range(1, lines):
            along(a, s).wait_recv()
            across(a, s).start()

    def assemble(a, whole, out):
        for s in range(lines):
            across(a, s).wait_recv()
        for q in range(cols):
            loose[q] = slots[a, q].astype(F32)
            for j in range(strips):
                at = slice(j * LANES, (j + 1) * LANES)
                stage[q * few : (q + 1) * few, at] = loose[q, j * few : (j + 1) * few, :]
        whole[...] = stage[...].astype(BF16)
        keep = pltpu.make_async_copy(whole, out, out_sem.at[a])
        keep.start()
        return keep

    def spread(i, k, value):
        for h in range(2):
            parts[k, h, i] = value[:, h * half : (h + 1) * half]

    def pair(m, k):
        at = pl.ds(0, 2) if m == 0 else 2
        return remote(
            parts.at[k, 1 - core, at], pair_recv.at[k, at], pair_ssem.at[m, k], pair_rsem.at[m, k], (partner, col)
        )

    def chip_copy(m, k, dy):
        at = pl.ds(0, 2) if m == 0 else 2
        to = ((chip + dy) % chips) * 2 + core
        return remote(
            chip_send.at[k, at], chip_recv.at[dy - 1, k, at],
            chip_ssem.at[m, dy - 1, k], chip_rsem.at[m, dy - 1, k], (to, col),
        )

    def share(k, owner):
        return remote(acts.at[k, owner], acts.at[k, owner], acts_ssem.at[k], acts_rsem.at[k], (partner, col))

    def forward_gu(k):
        at = slice(k * span, (k + 1) * span)
        spread(0, k, jnp.dot(tok_all[...], gate_buf[:, at], preferred_element_type=F32))
        spread(1, k, jnp.dot(tok_all[...], up_buf[:, at], preferred_element_type=F32))

    def forward_back(k):
        at = slice(k * span, (k + 1) * span)
        spread(2, k, lax.dot_general(down_buf[at, :], grad_all[...], LAST, preferred_element_type=F32).T)

    def chip_sum(m, k):
        for i in (0, 1) if m == 0 else (2,):
            total = parts[k, core, i] + pair_recv[k, i]
            parts[k, core, i] = total
            chip_send[k, i] = total.astype(BF16)

    def activate(k):
        sums = []
        for i in range(3):
            total = parts[k, core, i]
            for dy in range(1, chips):
                total += chip_recv[dy - 1, k, i].astype(F32)
            sums.append(total)
        for i, value in enumerate(hidden_grads(*sums)):
            acts[k, core, i] = value

    piece = depth // PIECES
    patch = strips // PIECES

    def contribution(k, at):
        value = None
        for h in range(2):
            cut = slice(k * span + h * half, k * span + (h + 1) * half)
            for i, buf in ((1, gate_buf), (2, up_buf)):
                term = lax.dot_general(buf[at, cut], acts[k, h, i], LAST, preferred_element_type=F32)
                value = term if value is None else value + term
        return value

    def scatter(b, s):
        to = (col + s) % cols
        return remote(dtok_send.at[b, to], dtok_recv.at[b, s], dtok_ssem.at[b, s], dtok_rsem.at[b, s], (row, to))

    def keep_acts(k):
        return pltpu.make_async_copy(acts.at[k], acts_out.at[k], acts_sem.at[k])

    def back_project(k):
        for b in range(2 * PIECES):
            at = slice(b * piece // 2, (b + 1) * piece // 2)
            value = contribution(k, at)
            acc[at, :] = value if k == 0 else acc[at, :] + value

    def finish(ks):
        for b in range(PIECES):
            for c in range(2):
                at = slice(b * piece + c * piece // 2, b * piece + (c + 1) * piece // 2)
                value = acc[at, :]
                for k in ks:
                    value += contribution(k, at)
                stage[:, at] = value.T
            for q in range(cols):
                for j in range(patch):
                    at = slice(b * piece + j * LANES, b * piece + (j + 1) * LANES)
                    loose[q, j * few : (j + 1) * few, :] = stage[q * few : (q + 1) * few, at]
                dtok_send[b, q] = loose[q, : patch * few, :].astype(BF16)
            for s in range(1, cols):
                scatter(b, s).start()

    keeps = [assemble(0, tok_all, tok_out)]
    last = chunks + LEAD - 1
    for s in range(chunks + LEAD + DELAY + 2):
        if s <= last:
            if s < chunks:
                load(0, s).wait()
                load(1, s).wait()
            if s == LEAD:
                keeps.append(assemble(1, grad_all, grad_out))
            if s >= LEAD:
                load(2, s - LEAD).wait()
            if s < chunks:
                forward_gu(s)
            if s >= LEAD:
                forward_back(s - LEAD)
            if s < chunks:
                pair(0, s).start()
            if s >= LEAD:
                pair(1, s - LEAD).start()
        sums = [(m, k) for m, k in ((0, s - 1), (1, s - 1 - LEAD)) if 0 <= k < chunks]
        for m, k in sums:
            pair(m, k).wait_recv()
        k = s - LEAD - 1 - DELAY
        if 0 <= k < chunks:
            for m in range(2):
                for dy in range(1, chips):
                    chip_copy(m, k, dy).wait_recv()
        for m, j in sums:
            chip_sum(m, j)
        for m, j in sums:
            for dy in range(1, chips):
                chip_copy(m, j, dy).start()
        if 0 <= k < chunks:
            activate(k)
            share(k, core).start()
        k -= 1
        if 0 <= k < chunks:
            share(k, 1 - core).wait_recv()
            keep_acts(k).start()
            if k < chunks - TAIL:
                back_project(k)
    finish(range(chunks - TAIL, chunks))

    for b in range(PIECES):
        result = dtok_send[b, col].astype(F32)
        for s in range(1, cols):
            scatter(b, s).wait_recv()
            result += dtok_recv[b, s].astype(F32)
        loose[b, : patch * few, :] = result
        for j in range(patch):
            at = slice(b * piece + j * LANES, b * piece + (j + 1) * LANES)
            stage[:few, at] = loose[b, j * few : (j + 1) * few, :]
    dtok_out[...] = stage[:few, :].astype(BF16)

    for copy in keeps:
        copy.wait()
    for a in range(2):
        for s in range(1, lines):
            along(a, s).wait_send()
        for s in range(lines):
            across(a, s).wait_send()
    for k in range(chunks):
        keep_acts(k).wait()
        share(k, core).wait_send()
        for m in range(2):
            pair(m, k).wait_send()
            for dy in range(1, chips):
                chip_copy(m, k, dy).wait_send()
    for b in range(PIECES):
        for s in range(1, cols):
            scatter(b, s).wait_send()


def exchange(rows, cols, tokens, grad_out, gate_weight, up_weight, down_weight):
    few, depth = tokens.shape
    hidden = gate_weight.shape[1]
    many = few * cols
    chips, lines = rows // 2, cols // 2
    chunks = hidden // (2 * HALF)
    bundle = few * depth // LANES
    dma = pltpu.SemaphoreType.DMA
    any_spec = pl.BlockSpec(memory_space=pl.ANY)
    vmem_spec = pl.BlockSpec(memory_space=pltpu.VMEM)
    shape = jax.ShapeDtypeStruct
    return pl.pallas_call(
        functools.partial(exchange_kernel, rows, cols),
        out_shape=(
            shape((many, depth), BF16),
            shape((many, depth), BF16),
            shape((chunks, 2, 3, many, HALF), BF16),
            shape((few, depth), BF16),
        ),
        in_specs=[vmem_spec, vmem_spec, any_spec, any_spec, any_spec],
        out_specs=(any_spec, any_spec, any_spec, vmem_spec),
        scratch_shapes=[
            pltpu.VMEM((depth, hidden), BF16),
            pltpu.VMEM((depth, hidden), BF16),
            pltpu.VMEM((hidden, depth), BF16),
            pltpu.VMEM((many, depth), BF16),
            pltpu.VMEM((many, depth), BF16),
            pltpu.VMEM((2, bundle, LANES), BF16),
            pltpu.VMEM((2, cols, bundle, LANES), BF16),
            pltpu.VMEM((cols, bundle, LANES), F32),
            pltpu.VMEM((many, depth), F32),
            pltpu.VMEM((chunks, 2, 3, many, HALF), F32),
            pltpu.VMEM((chunks, 3, many, HALF), F32),
            pltpu.VMEM((chunks, 3, many, HALF), BF16),
            pltpu.VMEM((chips - 1, chunks, 3, many, HALF), BF16),
            pltpu.VMEM((chunks, 2, 3, many, HALF), BF16),
            pltpu.VMEM((depth, many), F32),
            pltpu.VMEM((PIECES, cols, bundle // PIECES, LANES), BF16),
            pltpu.VMEM((PIECES, cols, bundle // PIECES, LANES), BF16),
            dma((3, chunks)),
            dma((2, lines)),
            dma((2, lines)),
            dma((2, lines)),
            dma((2, lines)),
            dma((2, chunks)),
            dma((2, chunks)),
            dma((2, chips - 1, chunks)),
            dma((2, chips - 1, chunks)),
            dma((chunks,)),
            dma((chunks,)),
            dma((PIECES, cols)),
            dma((PIECES, cols)),
            dma((2,)),
            dma((chunks,)),
        ],
        compiler_params=pltpu.CompilerParams(
            collective_id=0, has_side_effects=True, vmem_limit_bytes=62 * 1024 * 1024
        ),
        name="exchange",
    )(tokens, grad_out, gate_weight, up_weight, down_weight)


def outer_kernel(
    steps, tok_hbm, grad_hbm, acts_hbm, dtok, dtok_out, gate_hbm, up_hbm, down_hbm,
    tok, grad, acts, tok_t, hidden_t, gate_buf, up_buf, down_buf, in_sem, sem,
):
    chunks, _, _, _, half = acts.shape
    depth = tok.shape[1]
    hidden = chunks * 2 * half
    part, strip = depth // steps, hidden // steps

    ins = [
        pltpu.make_async_copy(src, dst, in_sem.at[n])
        for n, (src, dst) in enumerate(((tok_hbm, tok), (acts_hbm, acts), (grad_hbm, grad)))
    ]
    for copy in ins:
        copy.start()

    def copies(slot, t):
        over = pl.ds(pl.multiple_of(t * part, part), part)
        down = pl.ds(pl.multiple_of(t * strip, 16), strip)
        return (
            pltpu.make_async_copy(gate_buf.at[slot], gate_hbm.at[over, :], sem.at[0, slot]),
            pltpu.make_async_copy(up_buf.at[slot], up_hbm.at[over, :], sem.at[1, slot]),
            pltpu.make_async_copy(down_buf.at[slot], down_hbm.at[down, :], sem.at[2, slot]),
        )

    dtok_out[...] = dtok[...]
    ins[0].wait()
    tok_t[...] = tok[...].astype(F32).T.astype(BF16)
    ins[1].wait()
    ins[2].wait()

    @pl.loop(0, steps)
    def _(t):
        slot = t % 2
        over = pl.ds(pl.multiple_of(t * part, part), part)
        down = pl.ds(pl.multiple_of(t * strip, 16), strip)
        outs = copies(slot, t)

        @pl.when(t >= 2)
        def _():
            for copy in outs:
                copy.wait()

        for n, (buf, i) in enumerate(((gate_buf, 1), (up_buf, 2))):
            for k in range(chunks):
                for h in range(2):
                    at = slice((2 * k + h) * half, (2 * k + h + 1) * half)
                    buf[slot, :, at] = jnp.dot(
                        tok_t[over, :], acts[k, h, i], preferred_element_type=F32
                    ).astype(BF16)
            outs[n].start()

        @pl.when(t == 0)
        def _():
            for k in range(chunks):
                for h in range(2):
                    at = slice((2 * k + h) * half, (2 * k + h + 1) * half)
                    hidden_t[at, :] = acts[k, h, 0].astype(F32).T.astype(BF16)

        down_buf[slot] = jnp.dot(hidden_t[down, :], grad[...], preferred_element_type=F32).astype(BF16)
        outs[2].start()

    for slot in range(2):
        for copy in copies(slot, steps - 2 + slot):
            copy.wait()


def outer(tok, grad, acts, dtok):
    many, depth = tok.shape
    chunks, _, _, _, half = acts.shape
    hidden = chunks * 2 * half
    steps = 8
    shape = jax.ShapeDtypeStruct
    any_spec = pl.BlockSpec(memory_space=pl.ANY)
    vmem_spec = pl.BlockSpec(memory_space=pltpu.VMEM)
    return pl.pallas_call(
        functools.partial(outer_kernel, steps),
        out_shape=(
            shape(dtok.shape, BF16),
            shape((depth, hidden), BF16),
            shape((depth, hidden), BF16),
            shape((hidden, depth), BF16),
        ),
        in_specs=[any_spec, any_spec, any_spec, vmem_spec],
        out_specs=(vmem_spec, any_spec, any_spec, any_spec),
        scratch_shapes=[
            pltpu.VMEM((many, depth), BF16),
            pltpu.VMEM((many, depth), BF16),
            pltpu.VMEM(acts.shape, BF16),
            pltpu.VMEM((depth, many), BF16),
            pltpu.VMEM((hidden, many), BF16),
            pltpu.VMEM((2, depth // steps, hidden), BF16),
            pltpu.VMEM((2, depth // steps, hidden), BF16),
            pltpu.VMEM((2, hidden // steps, depth), BF16),
            pltpu.SemaphoreType.DMA((3,)),
            pltpu.SemaphoreType.DMA((3, 2)),
        ],
        compiler_params=pltpu.CompilerParams(vmem_limit_bytes=62 * 1024 * 1024),
        name="outer",
    )(tok, grad, acts, dtok)


def shards(rows, cols, tokens, grad_out, gate_weight, up_weight, down_weight):
    tok, grad, acts, grad_tokens = exchange(
        rows, cols, tokens, grad_out, gate_weight, up_weight, down_weight
    )
    return outer(tok, grad, acts, grad_tokens)


def plain_shards(tokens, grad_out, gate_weight, up_weight, down_weight):
    tok_full, grad_full = (
        lax.all_gather(tokens, "col", axis=0, tiled=True),
        lax.all_gather(grad_out, "col", axis=0, tiled=True),
    )
    hidden_width = gate_weight.shape[1]
    gate_part = jnp.dot(tok_full, gate_weight, preferred_element_type=F32)
    up_part = jnp.dot(tok_full, up_weight, preferred_element_type=F32)
    back_part = jnp.einsum("td,fd->tf", grad_full, down_weight, preferred_element_type=F32)
    sums = lax.psum(jnp.concatenate([gate_part, up_part, back_part], axis=1), "row")
    hidden, grad_gate, grad_up = hidden_grads(*jnp.split(sums, 3, axis=1))
    grad_down_weight = jnp.einsum("tf,td->fd", hidden, grad_full, preferred_element_type=F32).astype(BF16)
    grad_gate_weight = jnp.einsum("td,tf->df", tok_full, grad_gate, preferred_element_type=F32).astype(BF16)
    grad_up_weight = jnp.einsum("td,tf->df", tok_full, grad_up, preferred_element_type=F32).astype(BF16)
    total = jnp.einsum("tf,df->td", grad_gate, gate_weight, preferred_element_type=F32)
    total += jnp.einsum("tf,df->td", grad_up, up_weight, preferred_element_type=F32)
    grad_tokens = lax.psum_scatter(total, "col", scatter_dimension=0, tiled=True).astype(BF16)
    return (grad_tokens, grad_gate_weight, grad_up_weight, grad_down_weight)


def choose(rows, cols, *operands):
    depth, hidden = operands[2].shape
    if hidden % (2 * HALF) or depth % (PIECES * 2 * 128) or rows % 2 or cols % 2 or rows < 4:
        return plain_shards(*operands)
    return shards(rows, cols, *operands)


def solution(mesh):
    placed = (P("col", "row"), P("col", "row"), P("row", "col"), P("row", "col"), P("col", "row"))
    return jax.shard_map(
        functools.partial(choose, mesh.shape["row"], mesh.shape["col"]),
        mesh=mesh,
        in_specs=placed,
        out_specs=(P("col", "row"), P("row", "col"), P("row", "col"), P("col", "row")),
        check_vma=False,
    )
```

time: 88.2 us -> 61.9 us (0.70)
  Pallas kernels: 82.9 us -> 60.8 us
  local copies, waits for them, and re-layouts: 4.36 us -> 0 us
    pallas_call x1, Pallas kernels: 32.2 us -> 17.9 us  [outer(): pl.pallas_call(functools.partial(outer_kernel, steps), out_shape=(shape(d...]
    pallas_call x1, Pallas kernels: 50.7 us -> 42.9 us  [exchange(): pl.pallas_call(functools.partial(exchange_kernel, rows, cols), out_shape=...]
    unnamed x7 -> x0, local copies, waits for them, and re-layouts: 4.36 us -> none
where the time goes in v1:
time: 61.9 us; the launch traced here: 61.6 us
  Pallas kernels  60.8 us (98%)
  between operations  0.8 us (1%)
    pallas_call x1, Pallas kernels, exchange(): pl.pallas_call(functools.partial(exchange_kernel, rows, cols), out_shape=...  42.9 us
    pallas_call x1, Pallas kernels, outer(): pl.pallas_call(functools.partial(outer_kernel, steps), out_shape=(shape(d...  17.9 us

profile of v1, /device:TPU:0, one launch (start us, length us, event | category | flops | bytes accessed | tf_op | source)
XLA Modules:
  0.0 61.6 jit_solution(5720474911698142)
XLA Ops:
  0.6 42.9 %exchange.1 = (bf16[40,2048]{1,0:T(8,128)(2,1)}, bf16[40,2048]{1,0:T(8,128)(2,1)}, bf16[7,2,3,40,256]{4,3,2,1,0:T(8,128)(2,1)}, bf16[5,2048]{1,0:T(8,128)(2,1)}) custom-call(bf16[5,2048]{1,0:T(8,128)(2,1)} %tok_in.1, bf16[5,2048]{1,0:T(8,128)(2,1)} %grad_in.1, bf16[2048,3584]{1,0:T(8,128)(2,1)} %gate_hbm.1, bf16[2048,3584]{1,0:T(8,128)(2,1)} %up_hbm.1, ...), custom_call_target="tpu_custom_call" | custom-call | tf_op jit(solution)/shard_map/exchange/pallas_call | solution.py:290
  43.5 17.9 %outer.1 = (bf16[5,2048]{1,0:T(8,128)(2,1)}, bf16[2048,3584]{1,0:T(8,128)(2,1)}, bf16[2048,3584]{1,0:T(8,128)(2,1)}, bf16[3584,2048]{1,0:T(8,128)(2,1)}) custom-call(bf16[40,2048]{1,0:T(8,128)(2,1)} %get-tuple-element.8.tok_hbm, bf16[40,2048]{1,0:T(8,128)(2,1)} %get-tuple-element.9.grad_hbm, bf16[7,2,3,40,256]{4,3,2,1,0:T(8,128)(2,1)} %get-tuple-element.10.acts_hbm, ...), custom_call_target="tpu_custom_call" | custom-call | tf_op jit(solution)/shard_map/outer/pallas_call | solution.py:416

commit v2 on v1

--- a/solution.py
+++ b/solution.py
@@ -15,8 +15,8 @@
 LANES = 128
 LEAD = 2
 DELAY = 3
-PIECES = 2
-TAIL = 2
+PIECES = 4
+TAIL = 1
 
 
 def hidden_grads(gate_sum, up_sum, back_sum):
@@ -30,12 +30,12 @@
 
 
 def exchange_kernel(
-    rows, cols, tok_in, grad_in, gate_hbm, up_hbm, down_hbm,
+    rows, cols, tok_hbm, grad_hbm, gate_hbm, up_hbm, down_hbm,
     tok_out, grad_out, acts_out, dtok_out,
-    gate_buf, up_buf, down_buf, tok_all, grad_all, packed, slots, loose, stage, parts, pair_recv,
+    tok_in, grad_in, gate_buf, up_buf, down_buf, tok_all, grad_all, packed, slots, loose, stage, parts, pair_recv,
     chip_send, chip_recv, acts, acc, dtok_send, dtok_recv,
     load_sem, line_ssem, line_rsem, fwd_ssem, fwd_rsem, pair_ssem, pair_rsem,
-    chip_ssem, chip_rsem, acts_ssem, acts_rsem, dtok_ssem, dtok_rsem, out_sem, acts_sem,
+    chip_ssem, chip_rsem, acts_ssem, acts_rsem, dtok_ssem, dtok_rsem, in_sem, out_sem, acts_sem,
 ):
     row, col = lax.axis_index("row"), lax.axis_index("col")
     chips, lines = rows // 2, cols // 2
@@ -60,22 +60,29 @@
         src, dst = ((gate_hbm, gate_buf), (up_hbm, up_buf))[i]
         return pltpu.make_async_copy(src.at[:, at], dst.at[:, at], load_sem.at[i, k])
 
+    fetches = [
+        pltpu.make_async_copy(tok_hbm, tok_in, in_sem.at[0]),
+        pltpu.make_async_copy(grad_hbm, grad_in, in_sem.at[1]),
+    ]
+    for copy in fetches:
+        copy.start()
+
     order = []
     for s in range(chunks + LEAD):
         if s < chunks:
             order += [(0, s), (1, s)]
         if s >= LEAD:
             order.append((2, s - LEAD))
-    early = 2 * LEAD
-    for i, k in order[:early]:
-        load(i, k).start()
-
     barrier = pltpu.get_barrier_semaphore()
     for to in [partner] + [((chip + dy) % chips) * 2 + core for dy in range(1, chips)]:
         pl.semaphore_signal(barrier, inc=1, device_id=(to, col), device_id_type=MESH)
     for s in range(1, cols):
         pl.semaphore_signal(barrier, inc=1, device_id=(row, (col + s) % cols), device_id_type=MESH)
+    early = len(order) // 2
+    for i, k in order[:early]:
+        load(i, k).start()
     for a, whole in enumerate((tok_in, grad_in)):
+        fetches[a].wait()
         for j in range(strips):
             loose[a, j * few : (j + 1) * few, :] = whole[:, j * LANES : (j + 1) * LANES].astype(F32)
         mine = loose[a].astype(BF16)
@@ -83,17 +90,23 @@
         slots[a, col] = mine
     pl.semaphore_wait(barrier, chips + cols - 1)
 
+    def mate(s):
+        if lines != 4:
+            return (line + s) % lines, (line + lines - s) % lines
+        to = (line + 1 - 2 * (line % 2), (line + 2) % 4, 3 - line)[s - 1]
+        return to, to
+
     def along(a, s):
-        to = ((line + s) % lines) * 2 + side
+        to = mate(s)[0] * 2 + side
         return remote(packed.at[a], slots.at[a, col], line_ssem.at[a, s], line_rsem.at[a, s], (row, to))
 
     def across(a, s):
-        q = ((line + lines - s) % lines) * 2 + side
+        q = col if s == 0 else mate(s)[1] * 2 + side
         src = packed.at[a] if s == 0 else slots.at[a, q]
         return remote(src, slots.at[a, q], fwd_ssem.at[a, s], fwd_rsem.at[a, s], (row, line * 2 + 1 - side))
 
     for a in range(2):
-        for s in range(1, lines):
+        for s in range(lines - 1, 0, -1):
             along(a, s).start()
         across(a, 0).start()
     for i, k in order[early:]:
@@ -145,6 +158,24 @@
     def forward_back(k):
         at = slice(k * span, (k + 1) * span)
         spread(2, k, lax.dot_general(down_buf[at, :], grad_all[...], LAST, preferred_element_type=F32).T)
+
+    def forward_both(k, j):
+        for h in range(2):
+            at = slice(k * span + h * half, k * span + (h + 1) * half)
+            down = slice(j * span + h * half, j * span + (h + 1) * half)
+            gate_part = back_part = None
+            for d in range(0, depth, half):
+                cut = slice(d, d + half)
+                back_term = lax.dot_general(
+                    down_buf[down, cut], grad_all[:, cut], LAST, preferred_element_type=F32
+                )
+                gate_term = jnp.dot(tok_all[:, cut], gate_buf[cut, at], preferred_element_type=F32)
+                gate_part = gate_term if d == 0 else gate_part + gate_term
+                back_part = back_term if d == 0 else back_part + back_term
+            parts[k, h, 0] = gate_part
+            parts[j, h, 2] = back_part.T
+        at = slice(k * span, (k + 1) * span)
+        spread(1, k, jnp.dot(tok_all[...], up_buf[:, at], preferred_element_type=F32))
 
     def chip_sum(m, k):
         for i in (0, 1) if m == 0 else (2,):
@@ -214,9 +245,11 @@
                 keeps.append(assemble(1, grad_all, grad_out))
             if s >= LEAD:
                 load(2, s - LEAD).wait()
-            if s < chunks:
+            if LEAD <= s < chunks:
+                forward_both(s, s - LEAD)
+            elif s < chunks:
                 forward_gu(s)
-            if s >= LEAD:
+            else:
                 forward_back(s - LEAD)
             if s < chunks:
                 pair(0, s).start()
@@ -225,17 +258,16 @@
         sums = [(m, k) for m, k in ((0, s - 1), (1, s - 1 - LEAD)) if 0 <= k < chunks]
         for m, k in sums:
             pair(m, k).wait_recv()
+        for m, j in sums:
+            chip_sum(m, j)
+        for m, j in sums:
+            for dy in range(1, chips):
+                chip_copy(m, j, dy).start()
         k = s - LEAD - 1 - DELAY
         if 0 <= k < chunks:
             for m in range(2):
                 for dy in range(1, chips):
                     chip_copy(m, k, dy).wait_recv()
-        for m, j in sums:
-            chip_sum(m, j)
-        for m, j in sums:
-            for dy in range(1, chips):
-                chip_copy(m, j, dy).start()
-        if 0 <= k < chunks:
             activate(k)
             share(k, core).start()
         k -= 1
@@ -295,9 +327,11 @@
             shape((chunks, 2, 3, many, HALF), BF16),
             shape((few, depth), BF16),
         ),
-        in_specs=[vmem_spec, vmem_spec, any_spec, any_spec, any_spec],
+        in_specs=[any_spec] * 5,
         out_specs=(any_spec, any_spec, any_spec, vmem_spec),
         scratch_shapes=[
+            pltpu.VMEM((few, depth), BF16),
+            pltpu.VMEM((few, depth), BF16),
             pltpu.VMEM((depth, hidden), BF16),
             pltpu.VMEM((depth, hidden), BF16),
             pltpu.VMEM((hidden, depth), BF16),
@@ -329,6 +363,7 @@
             dma((PIECES, cols)),
             dma((PIECES, cols)),
             dma((2,)),
+            dma((2,)),
             dma((chunks,)),
         ],
         compiler_params=pltpu.CompilerParams(
@@ -339,8 +374,8 @@
 
 
 def outer_kernel(
-    steps, tok_hbm, grad_hbm, acts_hbm, dtok, dtok_out, gate_hbm, up_hbm, down_hbm,
-    tok, grad, acts, tok_t, hidden_t, gate_buf, up_buf, down_buf, in_sem, sem,
+    steps, tok_hbm, grad_hbm, acts_hbm, dtok_hbm, dtok_out, gate_hbm, up_hbm, down_hbm,
+    tok, grad, acts, dtok, tok_t, hidden_t, gate_buf, up_buf, down_buf, in_sem, sem,
 ):
     chunks, _, _, _, half = acts.shape
     depth = tok.shape[1]
@@ -349,39 +384,33 @@
 
     ins = [
         pltpu.make_async_copy(src, dst, in_sem.at[n])
-        for n, (src, dst) in enumerate(((tok_hbm, tok), (acts_hbm, acts), (grad_hbm, grad)))
+        for n, (src, dst) in enumerate(((tok_hbm, tok), (acts_hbm, acts), (grad_hbm, grad), (dtok_hbm, dtok)))
     ]
     for copy in ins:
         copy.start()
 
     def copies(slot, t):
-        over = pl.ds(pl.multiple_of(t * part, part), part)
         down = pl.ds(pl.multiple_of(t * strip, 16), strip)
+        whole = pl.ds(pl.multiple_of(t * part, part), part)
         return (
-            pltpu.make_async_copy(gate_buf.at[slot], gate_hbm.at[over, :], sem.at[0, slot]),
-            pltpu.make_async_copy(up_buf.at[slot], up_hbm.at[over, :], sem.at[1, slot]),
+            pltpu.make_async_copy(gate_buf.at[slot], gate_hbm.at[whole, :], sem.at[0, slot]),
+            pltpu.make_async_copy(up_buf.at[slot], up_hbm.at[whole, :], sem.at[1, slot]),
             pltpu.make_async_copy(down_buf.at[slot], down_hbm.at[down, :], sem.at[2, slot]),
         )
 
-    dtok_out[...] = dtok[...]
     ins[0].wait()
     tok_t[...] = tok[...].astype(F32).T.astype(BF16)
     ins[1].wait()
-    ins[2].wait()
 
     @pl.loop(0, steps)
     def _(t):
         slot = t % 2
-        over = pl.ds(pl.multiple_of(t * part, part), part)
         down = pl.ds(pl.multiple_of(t * strip, 16), strip)
         outs = copies(slot, t)
 
-        @pl.when(t >= 2)
-        def _():
-            for copy in outs:
-                copy.wait()
-
+        over = pl.ds(pl.multiple_of(t * part, part), part)
         for n, (buf, i) in enumerate(((gate_buf, 1), (up_buf, 2))):
+            pl.when(t >= 2)(outs[n].wait)
             for k in range(chunks):
                 for h in range(2):
                     at = slice((2 * k + h) * half, (2 * k + h + 1) * half)
@@ -396,23 +425,27 @@
                 for h in range(2):
                     at = slice((2 * k + h) * half, (2 * k + h + 1) * half)
                     hidden_t[at, :] = acts[k, h, 0].astype(F32).T.astype(BF16)
-
+            ins[2].wait()
+            ins[3].wait()
+            pltpu.make_async_copy(dtok, dtok_out, in_sem.at[4]).start()
+
+        pl.when(t >= 2)(outs[2].wait)
         down_buf[slot] = jnp.dot(hidden_t[down, :], grad[...], preferred_element_type=F32).astype(BF16)
         outs[2].start()
 
     for slot in range(2):
         for copy in copies(slot, steps - 2 + slot):
             copy.wait()
+    pltpu.make_async_copy(dtok, dtok_out, in_sem.at[4]).wait()
 
 
 def outer(tok, grad, acts, dtok):
     many, depth = tok.shape
     chunks, _, _, _, half = acts.shape
     hidden = chunks * 2 * half
-    steps = 8
+    steps = 4
     shape = jax.ShapeDtypeStruct
     any_spec = pl.BlockSpec(memory_space=pl.ANY)
-    vmem_spec = pl.BlockSpec(memory_space=pltpu.VMEM)
     return pl.pallas_call(
         functools.partial(outer_kernel, steps),
         out_shape=(
@@ -421,18 +454,19 @@
             shape((depth, hidden), BF16),
             shape((hidden, depth), BF16),
         ),
-        in_specs=[any_spec, any_spec, any_spec, vmem_spec],
-        out_specs=(vmem_spec, any_spec, any_spec, any_spec),
+        in_specs=[any_spec] * 4,
+        out_specs=(any_spec,) * 4,
         scratch_shapes=[
             pltpu.VMEM((many, depth), BF16),
             pltpu.VMEM((many, depth), BF16),
             pltpu.VMEM(acts.shape, BF16),
+            pltpu.VMEM(dtok.shape, BF16),
             pltpu.VMEM((depth, many), BF16),
             pltpu.VMEM((hidden, many), BF16),
             pltpu.VMEM((2, depth // steps, hidden), BF16),
             pltpu.VMEM((2, depth // steps, hidden), BF16),
             pltpu.VMEM((2, hidden // steps, depth), BF16),
-            pltpu.SemaphoreType.DMA((3,)),
+            pltpu.SemaphoreType.DMA((5,)),
             pltpu.SemaphoreType.DMA((3, 2)),
         ],
         compiler_params=pltpu.CompilerParams(vmem_limit_bytes=62 * 1024 * 1024),
@@ -469,7 +503,7 @@
 
 def choose(rows, cols, *operands):
     depth, hidden = operands[2].shape
-    if hidden % (2 * HALF) or depth % (PIECES * 2 * 128) or rows % 2 or cols % 2 or rows < 4:
+    if hidden % (2 * HALF) or depth % (PIECES * 4 * 128) or rows % 2 or cols % 2 or rows < 4:
         return plain_shards(*operands)
     return shards(rows, cols, *operands)
 

time: 61.9 us -> 60.5 us (0.977)
  Pallas kernels: 60.8 us -> 59.5 us
    pallas_call x1, Pallas kernels: 17.9 us -> 16.7 us  [outer(): pl.pallas_call(functools.partial(outer_kernel, steps), out_shape=(shape(d...]
where the time goes in v2:
time: 60.5 us; the launch traced here: 60.3 us
  Pallas kernels  59.5 us (98%)
  between operations  0.8 us (1%)
    pallas_call x1, Pallas kernels, exchange(): pl.pallas_call(functools.partial(exchange_kernel, rows, cols), out_shape=...  42.8 us
    pallas_call x1, Pallas kernels, outer(): pl.pallas_call(functools.partial(outer_kernel, steps), out_shape=(shape(d...  16.7 us

profile of v2, /device:TPU:0, one launch (start us, length us, event | category | flops | bytes accessed | tf_op | source)
XLA Modules:
  0.0 60.3 jit_solution(14806232834551991875)
XLA Ops:
  0.6 42.8 %exchange.1 = (bf16[40,2048]{1,0:T(8,128)(2,1)}, bf16[40,2048]{1,0:T(8,128)(2,1)}, bf16[7,2,3,40,256]{4,3,2,1,0:T(8,128)(2,1)}, bf16[5,2048]{1,0:T(8,128)(2,1)}) custom-call(bf16[5,2048]{1,0:T(8,128)(2,1)} %tok_hbm.1, bf16[5,2048]{1,0:T(8,128)(2,1)} %grad_hbm.1, bf16[2048,3584]{1,0:T(8,128)(2,1)} %gate_hbm.1, bf16[2048,3584]{1,0:T(8,128)(2,1)} %up_hbm.1, ...), custom_call_target="tpu_custom_call" | custom-call | tf_op jit(solution)/shard_map/exchange/pallas_call | solution.py:322
  43.5 16.7 %outer.1 = (bf16[5,2048]{1,0:T(8,128)(2,1)}, bf16[2048,3584]{1,0:T(8,128)(2,1)}, bf16[2048,3584]{1,0:T(8,128)(2,1)}, bf16[3584,2048]{1,0:T(8,128)(2,1)}) custom-call(bf16[40,2048]{1,0:T(8,128)(2,1)} %get-tuple-element.8.tok_hbm, bf16[40,2048]{1,0:T(8,128)(2,1)} %get-tuple-element.9.grad_hbm, bf16[7,2,3,40,256]{4,3,2,1,0:T(8,128)(2,1)} %get-tuple-element.10.acts_hbm, ...), custom_call_target="tpu_custom_call" | custom-call | tf_op jit(solution)/shard_map/outer/pallas_call | solution.py:449
